TPU v7x, 32 devices: a whole 2x2x4 slice. The times are simulated.
32 devices in a mesh: rows: 4 (over x, core), cols: 8 (over z, y).
Axes of the slice: x: 2, y: 2, z: 4, core: 2. Of those that a mesh axis runs over, the one named last changes fastest.
Arguments:
- samples: bfloat16 [2048, 65536], P('rows', 'cols'), may hold values from -0.0234375 to 0.0234375
- labels: int32 [2048], P('rows'), may hold values 0 or 1
- weights: float32 [65536], P('cols'), may hold values from -7 to 7, as said below
- hist_s: float32 [16, 65536], P(None, 'cols'), may hold values from -60 to 60
- hist_y: float32 [16, 65536], P(None, 'cols'), may hold values from -480 to 480, as said below
- counter: int32 [1], replicated, may hold values from 0 to 4095
Outputs:
- new_weights: float32 [65536], P('cols')
- gradient: float32 [65536], P('cols')
Inputs may be any that keep to these rules, and one draw needn't show every extreme that they name: weights share a common direction with the rows of hist_s. Each entry of hist_y[j] is a positive multiple of the same entry of hist_s[j], so s_j . y_j > 0.
All inputs are finite; a program needn't handle non-finite values. No bound on the sum of `labels` on one device may be relied on, other than what follows from the above.
Results may differ from a plain program's by a relative error of at most 0.0013.
Values sent between devices are 32-bit elements; how exact they have to be, the bound alone decides.
A program may use at most 64 MiB of HBM per device.

v0:
```python
import jax
import jax.numpy as jnp
from jax import lax
from jax.sharding import PartitionSpec as P

HIST = 16
penalty = 4.0
step_length = 0.5
highest = lax.Precision.HIGHEST


def row_share(values):
    width = values.shape[-1] // lax.axis_size("rows")
    return lax.dynamic_slice_in_dim(values, lax.axis_index("rows") * width, width, values.ndim - 1)


def quad_form(left, matrix, right):
    return jnp.dot(left, jnp.dot(matrix, right, precision=highest), precision=highest)


def gram_recursion(gram, basis, newest):
    count = 2 * HIST + 1
    places = jnp.arange(count, dtype=jnp.int32)
    select_s = (places == newest).astype(jnp.float32)
    select_y = (places == newest + HIST).astype(jnp.float32)
    gamma = quad_form(select_s, gram, select_y) / quad_form(select_y, gram, select_y)
    weights_of = (places == 2 * HIST).astype(jnp.float32)
    coefs = []
    pairs = []
    for step in range(HIST):
        slot = (newest - step) % HIST
        pick_s = (places == slot).astype(jnp.float32)
        pick_y = (places == slot + HIST).astype(jnp.float32)
        rho = 1.0 / quad_form(pick_s, gram, pick_y)
        coef = rho * quad_form(pick_s, gram, weights_of)
        coefs.append(coef)
        pairs.append((pick_s, pick_y, rho))
        weights_of = weights_of - coef * pick_y
    result_of = gamma * weights_of
    for step in reversed(range(HIST)):
        pick_s, pick_y, rho = pairs[step]
        beta = rho * quad_form(pick_y, gram, result_of)
        result_of = result_of + (coefs[step] - beta) * pick_s
    return jnp.dot(result_of, basis, precision=highest)


def body(samples, labels, weights, hist_s, hist_y, counter):
    margin_part = jnp.dot(samples, weights.astype(jnp.bfloat16), preferred_element_type=jnp.float32)
    margin = lax.psum(margin_part, "cols")
    resid = (jax.nn.sigmoid(margin) - labels.astype(jnp.float32)).astype(jnp.bfloat16)
    total_part = jnp.dot(resid, samples, preferred_element_type=jnp.float32)
    newest = counter[0] % HIST
    total = lax.psum(total_part, "rows")
    gradient = weights + penalty * total
    basis = jnp.concatenate([hist_s, hist_y, gradient[None, :]], axis=0)
    narrow_basis = row_share(basis)
    gram_part = jnp.dot(
        narrow_basis, narrow_basis.T, precision=highest, preferred_element_type=jnp.float32
    )
    gram = lax.psum(gram_part, ("rows", "cols"))
    result = gram_recursion(gram, basis, newest)
    return (weights - step_length * result, gradient)


def solution(mesh):
    in_specs = (P("rows", "cols"), P("rows"), P("cols"), P(None, "cols"), P(None, "cols"), P())
    out_specs = (P("cols"), P("cols"))
    return jax.shard_map(body, mesh=mesh, in_specs=in_specs, out_specs=out_specs, check_vma=False)
```

profile of v0, /device:TPU:14, one launch (start us, length us, event | category | flops | bytes accessed | tf_op | source)
XLA Modules:
  0.0 156.8 jit_solution(8693725162735482173)
XLA Ops:
  0.6 0.8 convert_element_type.8
  1.4 5.6 %fusion.186 = f32[1,512]{1,0:T(1,128)S(1)} fusion(bf16[512,8192]{1,0:T(8,128)(2,1)} %param.6, bf16[8192,1]{0,1:T(2,128)(2,1)S(1)} %reshape.4), kind=kOutput, calls=%fused_computation.303 | convolution fusion | flops 8388608 | bytes 8407040 | tf_op jit(solution)/shard_map/dot_general | solution.py:48
  7.1 15.2 %psum.21 = f32[512]{0:T(512)S(1)} all-reduce(f32[512]{0:T(512)S(1)} %bitcast.507), channel_id=1, replica_groups=mesh['rows'=4,'cols'=8] {'cols'}, use_global_device_ids=true, to_apply=%region_0.0 | all-reduce | flops 512 | bytes 4096 | tf_op jit(solution)/shard_map/psum | solution.py:49
  22.3 4.7 %fusion.187 = f32[1,8192]{1,0:T(1,128)S(1)} fusion(bf16[512,1]{0,1:T(2,128)(2,1)S(1)} %reshape.6, bf16[512,8192]{1,0:T(8,128)(2,1)} %param.6), kind=kOutput, calls=%fused_computation.304 | convolution fusion | flops 8388608 | bytes 8422400 | tf_op jit(solution)/shard_map/dot_general | solution.py:51
  26.9 10.4 %psum.22 = f32[8192]{0:T(1024)S(1)} all-reduce(f32[8192]{0:T(1024)S(1)} %bitcast.505), channel_id=1, replica_groups=mesh['rows'=4,'cols'=8] {'rows'}, use_global_device_ids=true, to_apply=%region_1.2 | all-reduce | flops 8192 | bytes 65536 | tf_op jit(solution)/shard_map/psum | solution.py:53
  37.4 0.1 pad_maximum_fusion
  37.5 0.4 fusion.96
  37.9 45.6 %psum.23 = f32[33,33]{1,0:T(8,128)S(1)} all-reduce(f32[33,33]{1,0:T(8,128)S(1)} %fusion.96), channel_id=1, replica_groups=mesh['rows'=4,'cols'=8] {'rows','cols'}, use_global_device_ids=true, to_apply=%region_2.3 | all-reduce | flops 1089 | bytes 8712 | tf_op jit(solution)/shard_map/psum | solution.py:60
  84.2 0.7 fusion.48
  85.7 0.7 fusion.49
  87.1 0.7 fusion.50
  88.5 0.8 fusion.51
  90.0 0.7 fusion.52
  91.4 0.8 fusion.53
  92.8 0.7 fusion.56
  94.3 0.7 fusion.54
  95.7 0.8 fusion.55
  97.1 0.8 fusion.57
  98.6 0.7 fusion.60
  100.0 0.7 fusion.58
  101.5 0.8 fusion.59
  102.9 0.8 fusion.61
  104.3 0.7 fusion.64
  105.8 0.7 fusion.62
  107.2 0.8 fusion.63
  108.6 0.8 fusion.65
  110.1 0.7 fusion.68
  111.5 0.7 fusion.66
  113.0 0.8 fusion.67
  114.4 0.8 fusion.69
  115.8 0.7 fusion.72
  117.3 0.7 fusion.70
  118.7 0.8 fusion.71
  120.1 0.8 fusion.73
  121.6 0.7 fusion.76
  123.0 0.7 fusion.74
  124.5 0.8 fusion.75
  125.9 0.8 fusion.77
  127.3 0.7 fusion.78
  128.8 0.8 fusion.79
  130.2 0.8 fusion.121
  132.4 0.8 fusion.80
  133.8 0.8 fusion.81
  135.3 0.8 fusion.82
  136.7 0.8 fusion.83
  138.1 0.1 select_add_fusion.11
  138.2 0.8 fusion.84
  139.6 0.8 fusion.85
  141.0 0.1 select_add_fusion.9
  141.1 0.8 fusion.86
  142.5 0.8 fusion.87
  143.9 0.1 select_add_fusion.7
  144.0 0.8 fusion.88
  145.4 0.8 fusion.89
  146.8 0.1 select_add_fusion.5
  146.9 0.8 fusion.90
  148.3 0.8 fusion.91
  149.7 0.1 select_add_fusion.3
  149.8 0.8 fusion.92
  151.2 0.8 fusion.93
  152.6 0.8 fusion.94
  154.0 0.8 fusion.95
  155.4 0.7 fusion.124
  156.2 0.6 multiply_subtract_fusion
  (23 shorter events, 0.3 us)
Async XLA Ops:
  1.4 20.8 %copy-start.4 = (s32[512]{0:T(512)S(1)}, s32[512]{0:T(512)}, u32[]{:S(2)}) copy-start(s32[512]{0:T(512)} %param.7) | copy-start | bytes 6148
  22.2 15.1 %copy-start.2 = (f32[8192]{0:T(1024)S(1)}, f32[8192]{0:T(1024)}, u32[]{:S(2)}) copy-start(f32[8192]{0:T(1024)} %param.8) | copy-start | bytes 98308
  22.3 15.1 %copy-start = (f32[16,8192]{1,0:T(8,128)S(1)}, f32[16,8192]{1,0:T(8,128)}, u32[]{:S(2)}) copy-start(f32[16,8192]{1,0:T(8,128)} %param.10) | copy-start | bytes 1572868
  22.3 15.1 %copy-start.1 = (f32[16,8192]{1,0:T(8,128)S(1)}, f32[16,8192]{1,0:T(8,128)}, u32[]{:S(2)}) copy-start(f32[16,8192]{1,0:T(8,128)} %param.9) | copy-start | bytes 1572868
  37.4 118.1 %copy-start.3 = (f32[8192]{0:T(1024)}, f32[8192]{0:T(1024)S(1)}, u32[]{:S(2)}) copy-start(f32[8192]{0:T(1024)S(1)} %multiply_add_fusion) | copy-start | bytes 98308
where the time goes:
time: 158 us; the launch traced here: 157 us
  blocking collectives  71.2 us (45%)
  matrix products  48.3 us (31%)
  between operations  35.2 us (22%)
  other arithmetic  2.05 us (1%)
    psum x1, blocking collectives, body(): gram = lax.psum(gram_part, ('rows', 'cols'))  45.6 us
    dot_general x49, matrix products, quad_form(): jnp.dot(matrix, right, precision=highest)  36.8 us
    psum x1, blocking collectives, body(): margin = lax.psum(margin_part, 'cols')  15.2 us
    psum x1, blocking collectives, body(): total = lax.psum(total_part, 'rows')  10.4 us
    dot_general x1, matrix products, body(): jnp.dot(samples, weights.astype(jnp.bfloat16), preferred_element_type=jnp...  5.64 us
    dot_general x1, matrix products, body(): total_part = jnp.dot(resid, samples, preferred_element_type=jnp.float32)  4.66 us

commit v1 on v0

--- a/solution.py
+++ b/solution.py
@@ -46,7 +46,7 @@
 
 def body(samples, labels, weights, hist_s, hist_y, counter):
     margin_part = jnp.dot(samples, weights.astype(jnp.bfloat16), preferred_element_type=jnp.float32)
-    margin = lax.psum(margin_part, "cols")
+    margin = jnp.sum(lax.all_gather(margin_part, "cols"), axis=0)
     resid = (jax.nn.sigmoid(margin) - labels.astype(jnp.float32)).astype(jnp.bfloat16)
     total_part = jnp.dot(resid, samples, preferred_element_type=jnp.float32)
     newest = counter[0] % HIST

time: 158 us -> 164 us (1.038)
  blocking collectives: 71.2 us -> 76 us
    all_gather x0 -> x1, blocking collectives: none -> 25.2 us  [body(): margin = jnp.sum(lax.all_gather(margin_part, 'cols'), axis=0)]
    psum x1 -> x0, blocking collectives: 15.2 us -> none  [body(): margin = lax.psum(margin_part, 'cols')]
    psum x1, blocking collectives: 45.6 us -> 40.4 us  [body(): gram = lax.psum(gram_part, ('rows', 'cols'))]
where the time goes in v1:
time: 164 us; the launch traced here: 162 us
  blocking collectives  76 us (46%)
  matrix products  48.3 us (29%)
  between operations  35.3 us (22%)
  other arithmetic  2.08 us (1%)
    psum x1, blocking collectives, body(): gram = lax.psum(gram_part, ('rows', 'cols'))  40.4 us
    dot_general x49, matrix products, quad_form(): jnp.dot(matrix, right, precision=highest)  36.8 us
    all_gather x1, blocking collectives, body(): margin = jnp.sum(lax.all_gather(margin_part, 'cols'), axis=0)  25.2 us
    psum x1, blocking collectives, body(): total = lax.psum(total_part, 'rows')  10.4 us
    dot_general x1, matrix products, body(): jnp.dot(samples, weights.astype(jnp.bfloat16), preferred_element_type=jnp...  5.64 us
    dot_general x1, matrix products, body(): total_part = jnp.dot(resid, samples, preferred_element_type=jnp.float32)  4.66 us

profile of v1, /device:TPU:14, one launch (start us, length us, event | category | flops | bytes accessed | tf_op | source)
XLA Modules:
  0.0 161.6 jit_solution(2406613836114162533)
XLA Ops:
  0.6 0.8 convert_element_type.8
  1.4 5.6 %convolution_bitcast_fusion = f32[1,1,512]{2,1,0:T(1,128)S(1)} fusion(bf16[512,8192]{1,0:T(8,128)(2,1)} %param.6, bf16[8192,1]{0,1:T(2,128)(2,1)S(1)} %reshape.8), kind=kOutput, calls=%fused_computation.1 | convolution fusion | flops 8388608 | bytes 8407040 | tf_op jit(solution)/shard_map/dot_general | solution.py:48
  7.1 25.2 %all-gather.1 = f32[8,1,512]{2,1,0:T(1,128)S(1)} all-gather(f32[1,1,512]{2,1,0:T(1,128)S(1)} %convolution_bitcast_fusion), channel_id=2, replica_groups=mesh['rows'=4,'cols'=8] {'cols'}, dimensions={0}, use_global_device_ids=true | all-gather | bytes 18432 | tf_op jit(solution)/shard_map/all_gather | solution.py:49
  32.3 4.7 %fusion.186 = f32[1,8192]{1,0:T(1,128)S(1)} fusion(bf16[512,1]{0,1:T(2,128)(2,1)S(1)} %reshape.10, bf16[512,8192]{1,0:T(8,128)(2,1)} %param.6), kind=kOutput, calls=%fused_computation.304 | convolution fusion | flops 8388608 | bytes 8422400 | tf_op jit(solution)/shard_map/dot_general | solution.py:51
  37.0 10.4 %psum.14 = f32[8192]{0:T(1024)S(1)} all-reduce(f32[8192]{0:T(1024)S(1)} %bitcast.508), channel_id=1, replica_groups=mesh['rows'=4,'cols'=8] {'rows'}, use_global_device_ids=true, to_apply=%region_1.2 | all-reduce | flops 8192 | bytes 65536 | tf_op jit(solution)/shard_map/psum | solution.py:53
  47.4 0.1 pad_maximum_fusion
  47.5 0.4 fusion.96
  48.0 40.4 %psum.15 = f32[33,33]{1,0:T(8,128)S(1)} all-reduce(f32[33,33]{1,0:T(8,128)S(1)} %fusion.96), channel_id=1, replica_groups=mesh['rows'=4,'cols'=8] {'rows','cols'}, use_global_device_ids=true, to_apply=%region_2.3 | all-reduce | flops 1089 | bytes 8712 | tf_op jit(solution)/shard_map/psum | solution.py:60
  89.1 0.7 fusion.48
  90.5 0.7 fusion.49
  91.9 0.7 fusion.50
  93.3 0.8 fusion.51
  94.8 0.7 fusion.52
  96.2 0.8 fusion.53
  97.7 0.7 fusion.56
  99.1 0.7 fusion.54
  100.5 0.8 fusion.55
  102.0 0.8 fusion.57
  103.4 0.7 fusion.60
  104.9 0.7 fusion.58
  106.3 0.8 fusion.59
  107.7 0.8 fusion.61
  109.1 0.7 fusion.64
  110.6 0.7 fusion.62
  112.0 0.8 fusion.63
  113.5 0.8 fusion.65
  114.9 0.7 fusion.68
  116.3 0.7 fusion.66
  117.8 0.8 fusion.67
  119.2 0.8 fusion.69
  120.6 0.7 fusion.72
  122.1 0.7 fusion.70
  123.5 0.8 fusion.71
  125.0 0.8 fusion.73
  126.4 0.7 fusion.76
  127.8 0.7 fusion.74
  129.3 0.8 fusion.75
  130.7 0.8 fusion.77
  132.1 0.7 fusion.78
  133.6 0.8 fusion.79
  135.0 0.8 fusion.121
  137.3 0.8 fusion.80
  138.7 0.8 fusion.81
  140.1 0.8 fusion.82
  141.5 0.8 fusion.83
  143.0 0.1 select_add_fusion.11
  143.0 0.8 fusion.84
  144.4 0.8 fusion.85
  145.8 0.1 select_add_fusion.9
  145.9 0.8 fusion.86
  147.3 0.8 fusion.87
  148.7 0.1 select_add_fusion.7
  148.8 0.8 fusion.88
  150.2 0.8 fusion.89
  151.6 0.1 select_add_fusion.5
  151.7 0.8 fusion.90
  153.1 0.8 fusion.91
  154.5 0.1 select_add_fusion.3
  154.6 0.8 fusion.92
  156.0 0.8 fusion.93
  157.4 0.8 fusion.94
  158.8 0.8 fusion.95
  160.3 0.7 fusion.124
  161.0 0.6 multiply_subtract_fusion
  (24 shorter events, 0.3 us)
Async XLA Ops:
  1.4 30.8 %copy-start.4 = (s32[512]{0:T(512)S(1)}, s32[512]{0:T(512)}, u32[]{:S(2)}) copy-start(s32[512]{0:T(512)} %param.7) | copy-start | bytes 6148
  32.3 15.1 %copy-start.2 = (f32[8192]{0:T(1024)S(1)}, f32[8192]{0:T(1024)}, u32[]{:S(2)}) copy-start(f32[8192]{0:T(1024)} %param.8) | copy-start | bytes 98308
  32.3 15.1 %copy-start = (f32[16,8192]{1,0:T(8,128)S(1)}, f32[16,8192]{1,0:T(8,128)}, u32[]{:S(2)}) copy-start(f32[16,8192]{1,0:T(8,128)} %param.10) | copy-start | bytes 1572868
  32.3 15.1 %copy-start.1 = (f32[16,8192]{1,0:T(8,128)S(1)}, f32[16,8192]{1,0:T(8,128)}, u32[]{:S(2)}) copy-start(f32[16,8192]{1,0:T(8,128)} %param.9) | copy-start | bytes 1572868
  47.4 112.8 %copy-start.3 = (f32[8192]{0:T(1024)}, f32[8192]{0:T(1024)S(1)}, u32[]{:S(2)}) copy-start(f32[8192]{0:T(1024)S(1)} %multiply_add_fusion) | copy-start | bytes 98308
